TPU v7x, 32 devices: a whole 2x2x4 slice. The times are simulated.
32 devices in a mesh: grp: 2 (over y), shot: 4 (over x, core), slab: 4 (over z).
Axes of the slice: x: 2, y: 2, z: 4, core: 2. Of those that a mesh axis runs over, the one named last changes fastest.
Arguments:
- courant_sq: float32 [512, 1024], P(('grp', 'slab')), parts along dimension 0, may hold values from 0.05 to 0.25
- sponge_level: int32 [512, 1024], P(('grp', 'slab')), parts along dimension 0, may hold values from 0 to 3
- source_later: float32 [16, 256, 1024], P(('grp', 'shot'), 'slab'), parts along dimension 0, may hold values from -6 to 6
- source_now: float32 [16, 256, 1024], P(('grp', 'shot'), 'slab'), parts along dimension 0, may hold values from -6 to 6
- receiver_later: float32 [16, 256, 1024], P(('grp', 'shot'), 'slab'), parts along dimension 0, may hold values from -6 to 6
- receiver_now: float32 [16, 256, 1024], P(('grp', 'shot'), 'slab'), parts along dimension 0, may hold values from -6 to 6
- traces: float32 [16, 16, 512], P(('grp', 'shot')), parts along dimension 0, may hold values from -24 to 24
- wavelet: float32 [512], P('grp'), parts along dimension 0, may hold values from -24 to 24
- source_depth: int32 [16], P(('grp', 'shot')), parts along dimension 0, may hold values from 0 to 255
- source_lateral: int32 [16], P(('grp', 'shot')), parts along dimension 0, may hold values from 0 to 1023
- receiver_depth: int32 [16, 512], P(('grp', 'shot')), parts along dimension 0, may hold values from 0 to 255
- receiver_lateral: int32 [16, 512], P(('grp', 'shot')), parts along dimension 0, may hold values from 0 to 1023
- checkpoint_step: int32 [16], P(('grp', 'shot')), parts along dimension 0, may hold values from 0 to 240
Outputs:
- image: float32 [512, 1024], P(('grp', 'slab')), parts along dimension 0
- source_out: float32 [16, 256, 1024], P(('grp', 'shot'), 'slab'), parts along dimension 0
- receiver_out: float32 [16, 256, 1024], P(('grp', 'shot'), 'slab'), parts along dimension 0
There are 2 independent parts, one for each index of `grp`. A program takes and returns all parts, laid end to end along the dimension named above; each array names one. Nothing has to cross between parts.
All inputs are finite; a program needn't handle non-finite values.
Results may differ from a plain program's by a relative error of at most 0.0003.
Values sent between devices are 32-bit elements; how exact they have to be, the bound alone decides.
A program may use at most 64 MiB of HBM per device.

v0:
```python
import math

import jax
import jax.numpy as jnp
from jax import lax
from jax.sharding import PartitionSpec as P

STEPS = 16


stencil_coeffs = (-205.0 / 72.0, 8.0 / 5.0, -1.0 / 5.0, 8.0 / 315.0, -1.0 / 560.0)


def extended_2(cells, sides, width):
    for axis, dim in sides:
        count = lax.axis_size(axis)
        ends = count - 1
        head = lax.slice_in_dim(cells, 0, width, axis=dim)
        tail = lax.slice_in_dim(cells, cells.shape[dim] - width, cells.shape[dim], axis=dim)
        cells = jnp.concatenate(
            [
                lax.ppermute(tail, axis, [(i, (i + 1) % count) for i in range(ends)]),
                cells,
                lax.ppermute(head, axis, [((i + 1) % count, i) for i in range(ends)]),
            ],
            axis=dim,
        )
    return cells


def laplace(extended):
    row_count = extended.shape[-2] - 8
    width = extended.shape[-1]
    centre = extended[..., 4 : 4 + row_count, :]
    pad_spec = [(0, 0)] * (centre.ndim - 1) + [(4, 4)]
    padded = jnp.pad(centre, pad_spec)
    result = 2.0 * stencil_coeffs[0] * centre
    for offset in range(1, 5):
        result = result + stencil_coeffs[offset] * (
            extended[..., 4 + offset : 4 + offset + row_count, :]
            + extended[..., 4 - offset : 4 - offset + row_count, :]
            + padded[..., 4 + offset : 4 + offset + width]
            + padded[..., 4 - offset : 4 - offset + width]
        )
    return result


def local(
    courant_sq,
    sponge_level,
    source_later,
    source_now,
    receiver_later,
    receiver_now,
    traces,
    wavelet,
    source_depth,
    source_lateral,
    receiver_depth,
    receiver_lateral,
    checkpoint_step,
):
    slab_rows = courant_sq.shape[0]
    lateral_cells = courant_sq.shape[1]
    first_row = lax.axis_index("slab") * slab_rows
    damping = 1.0 - 0.06 * sponge_level.astype(jnp.float32)
    lateral_ids = jnp.arange(lateral_cells, dtype=jnp.int32)
    lateral_table = (receiver_lateral[:, :, None] == lateral_ids[None, None, :]).astype(jnp.float32)
    source_column = lateral_ids[None, :] == source_lateral[:, None]

    def advance(src_now, src_hi, rec_now, rec_hi, laplacian, velocity, damper, top_row, step_index):
        row_count = src_now.shape[1]
        row_ids = top_row + jnp.arange(row_count, dtype=jnp.int32)
        pulse = wavelet[checkpoint_step + STEPS - 1 - step_index]
        source_cell = (row_ids[None, :, None] == source_depth[:, None, None]) & source_column[
            :, None, :
        ]
        injected_src = jnp.where(source_cell, pulse[:, None, None], 0.0)
        src_next = 2.0 * src_now - src_hi + velocity * laplacian[0] - velocity * injected_src
        trace_now = lax.dynamic_index_in_dim(traces, step_index, 1, keepdims=False)
        depth_table = jnp.where(
            row_ids[None, :, None] == receiver_depth[:, None, :], trace_now[:, None, :], 0.0
        )
        injected_rec = jnp.einsum(
            "szr,srx->szx",
            depth_table,
            lateral_table,
            precision=lax.Precision.HIGHEST,
            preferred_element_type=jnp.float32,
        )
        rec_next = 2.0 * rec_now - rec_hi + velocity * laplacian[1] + velocity * injected_rec
        rec_next = damper * rec_next
        return (src_next, rec_next)

    start_image = jnp.zeros(courant_sq.shape, jnp.float32)
    model = extended_2(jnp.stack([courant_sq, damping]), (("slab", 1),), 8)
    velocity_wide = model[0, 4 : slab_rows + 12]
    damper_wide = model[1, 4 : slab_rows + 12]

    def pair_step(pair_index, carry):
        src_hi, src_now, rec_hi, rec_now, image_local = carry
        step_first = 2 * pair_index
        image_local = image_local + jnp.sum(src_now * rec_now, axis=0)
        extended = extended_2(jnp.stack([src_now, rec_now, src_hi, rec_hi]), (("slab", 2),), 8)
        laplacian = laplace(extended[0:2])
        src_wide = extended[0, :, 4 : slab_rows + 12]
        rec_wide = extended[1, :, 4 : slab_rows + 12]
        src_hi_wide = extended[2, :, 4 : slab_rows + 12]
        rec_hi_wide = extended[3, :, 4 : slab_rows + 12]
        src_mid, rec_mid = advance(
            src_wide,
            src_hi_wide,
            rec_wide,
            rec_hi_wide,
            laplacian,
            velocity_wide,
            damper_wide,
            first_row - 4,
            step_first,
        )
        src_centre = src_mid[:, 4 : slab_rows + 4]
        rec_centre = rec_mid[:, 4 : slab_rows + 4]
        image_local = image_local + jnp.sum(src_centre * rec_centre, axis=0)
        second = laplace(jnp.stack([src_mid, rec_mid]))
        src_last, rec_last = advance(
            src_centre,
            src_now,
            rec_centre,
            rec_now,
            second,
            courant_sq,
            damping,
            first_row,
            step_first + 1,
        )
        return (src_centre, src_last, rec_centre, rec_last, image_local)

    carry = lax.fori_loop(
        0,
        STEPS // 2,
        pair_step,
        (source_later, source_now, receiver_later, receiver_now, start_image),
    )
    source_final = carry[1]
    receiver_final = carry[3]
    image_total = lax.psum(carry[4], "shot")
    shots_all = lax.axis_size("shot") * source_now.shape[0]
    image = image_total / math.sqrt(STEPS * shots_all)
    return (image, source_final, receiver_final)


def solution(mesh):
    in_specs = (
        P(("grp", "slab"), None),
        P(("grp", "slab"), None),
        P(("grp", "shot"), "slab", None),
        P(("grp", "shot"), "slab", None),
        P(("grp", "shot"), "slab", None),
        P(("grp", "shot"), "slab", None),
        P(("grp", "shot"), None, None),
        P("grp"),
        P(("grp", "shot")),
        P(("grp", "shot")),
        P(("grp", "shot"), None),
        P(("grp", "shot"), None),
        P(("grp", "shot")),
    )
    out_specs = (
        P(("grp", "slab"), None),
        P(("grp", "shot"), "slab", None),
        P(("grp", "shot"), "slab", None),
    )
    return jax.shard_map(local, mesh=mesh, in_specs=in_specs, out_specs=out_specs, check_vma=False)
```

profile of v0, /device:TPU:0, one launch (start us, length us, event | category | flops | bytes accessed | tf_op | source)
XLA Modules:
  0.0 274.1 jit_solution(1386798049830185891)
XLA Ops:
  9.0 5.1 %collective-permute-start.2 = (f32[2,8,1024]{2,1,0:T(8,128)S(1)}, f32[2,8,1024]{2,1,0:T(8,128)S(1)}, u32[]{:S(2)}, u32[]{:S(2)}) collective-permute-start(f32[2,8,1024]{2,1,0:T(8,128)S(1)} %get-tuple-element.729), channel_id=1, source_target_pairs={{0,1},{1,2},{2,3},{4,5},{5,6},{6,7},{8,9},{9,10},{10,11},{12,13},{... | collective-permute-start | bytes 196616 | tf_op jit(solution)/shard_map/ppermute | solution.py:22
  16.0 4.3 %collective-permute-done.3 = f32[2,8,1024]{2,1,0:T(8,128)S(1)} collective-permute-done((f32[2,8,1024]{2,1,0:T(8,128)S(1)}, f32[2,8,1024]{2,1,0:T(8,128)S(1)}, u32[]{:S(2)}, u32[]{:S(2)}) %collective-permute-start.3) | collective-permute-done | bytes 65568 | tf_op jit(solution)/shard_map/ppermute | solution.py:24
  21.1 209.0 %while.26 = (s32[]{:T(128)}, f32[2,64,1024]{2,1,0:T(8,128)S(1)}, f32[2,64,1024]{2,1,0:T(8,128)S(1)}, f32[2,64,1024]{2,1,0:T(8,128)S(1)}, f32[2,64,1024]{2,1,0:T(...) while((s32[]{:T(128)}, f32[2,64,1024]{2,1,0:T(8,128)S(1)}, ...), condition=%wide.region_3.4_spmd.clone, body=%wide.region_0.3_spmd.clone.sunk | while | flops 1741394304 | bytes 51560036 | solution.py:138
  23.2 4.6 %collective-permute-start.1 = (f32[4,2,8,1024]{3,2,1,0:T(8,128)}, f32[4,2,8,1024]{3,2,1,0:T(8,128)S(1)}, u32[]{:S(2)}, u32[]{:S(2)}) collective-permute-start(f32[4,2,8,1024]{3,2,1,0:T(8,128)} %get-tuple-element.863), channel_id=1, source_target_pairs={{0,1},{1,2},{2,3},{4,5},{5,6},{6,7},{8,9},{9,10},{10,11},{12,13},{... | collective-permute-start | bytes 786440 | tf_op jit(solution)/shard_map/while/body/eval_jaxpr/ppermute | solution.py:22
  32.3 2.6 fusion.117
  35.9 3.2 %fusion.118 = f32[2,72,1024]{2,1,0:T(8,128)S(1)} fusion(f32[2,2,72,1024]{3,2,1,0:T(8,128)S(1)} %fusion.117, f32[4,2,80,1024]{3,2,1,0:T(8,128)S(1)} %pad_maximum_fusion.23, s32[2,512]{1,0:T(2,128)S(1)} %copy-done.17, f32[72,1024]{1,0:T(8,128)S(1)} %bitcast.101, f32[72,1024]{1,0:T(8,128)S(1)} %bitcast.98, f32[2,512]{1,0:T(2,128)S(1)} %get-tuple-element.864, ...), kind=kOutput, calls=%fused_computation.109.clone.1 | convolution fusion | flops 909246464 | bytes 2961696 | tf_op jit(solution)/shard_map/while/body/eval_jaxpr/szr,srx->szx/dot_general | solution.py:84
  39.2 2.4 fusion.121
  42.9 3.1 %fusion.122 = f32[2,64,1024]{2,1,0:T(8,128)S(1)} fusion(s32[2,512]{1,0:T(2,128)S(1)} %copy-done.17, f32[2,2,64,1024]{3,2,1,0:T(8,128)S(1)} %fusion.121, f32[2,64,1024]{2,1,0:T(8,128)S(1)} %get-tuple-element.904, f32[2,64,1024]{2,1,0:T(8,128)S(1)} %get-tuple-element.927, f32[64,1024]{1,0:T(8,128)S(1)} %copy-done.12, ...), kind=kOutput, calls=%fused_computation.39.clone.1 | convolution fusion | flops 808452096 | bytes 2633984 | tf_op jit(solution)/shard_map/while/body/eval_jaxpr/szr,srx->szx/dot_general | solution.py:84
  49.0 4.9 %collective-permute-start.1 = (f32[4,2,8,1024]{3,2,1,0:T(8,128)}, f32[4,2,8,1024]{3,2,1,0:T(8,128)S(1)}, u32[]{:S(2)}, u32[]{:S(2)}) collective-permute-start(f32[4,2,8,1024]{3,2,1,0:T(8,128)} %get-tuple-element.863), channel_id=1, source_target_pairs={{0,1},{1,2},{2,3},{4,5},{5,6},{6,7},{8,9},{9,10},{10,11},{12,13},{... | collective-permute-start | bytes 786440 | tf_op jit(solution)/shard_map/while/body/eval_jaxpr/ppermute | solution.py:22
  56.6 1.6 collective-permute-done.1
  58.5 2.6 fusion.117
  62.1 3.2 %fusion.118 = f32[2,72,1024]{2,1,0:T(8,128)S(1)} fusion(f32[2,2,72,1024]{3,2,1,0:T(8,128)S(1)} %fusion.117, f32[4,2,80,1024]{3,2,1,0:T(8,128)S(1)} %pad_maximum_fusion.23, s32[2,512]{1,0:T(2,128)S(1)} %copy-done.17, f32[72,1024]{1,0:T(8,128)S(1)} %bitcast.101, f32[72,1024]{1,0:T(8,128)S(1)} %bitcast.98, f32[2,512]{1,0:T(2,128)S(1)} %get-tuple-element.864, ...), kind=kOutput, calls=%fused_computation.109.clone.1 | convolution fusion | flops 909246464 | bytes 2961696 | tf_op jit(solution)/shard_map/while/body/eval_jaxpr/szr,srx->szx/dot_general | solution.py:84
  65.4 2.4 fusion.121
  69.1 3.1 %fusion.122 = f32[2,64,1024]{2,1,0:T(8,128)S(1)} fusion(s32[2,512]{1,0:T(2,128)S(1)} %copy-done.17, f32[2,2,64,1024]{3,2,1,0:T(8,128)S(1)} %fusion.121, f32[2,64,1024]{2,1,0:T(8,128)S(1)} %get-tuple-element.904, f32[2,64,1024]{2,1,0:T(8,128)S(1)} %get-tuple-element.927, f32[64,1024]{1,0:T(8,128)S(1)} %copy-done.12, ...), kind=kOutput, calls=%fused_computation.39.clone.1 | convolution fusion | flops 808452096 | bytes 2633984 | tf_op jit(solution)/shard_map/while/body/eval_jaxpr/szr,srx->szx/dot_general | solution.py:84
  75.2 4.9 %collective-permute-start.1 = (f32[4,2,8,1024]{3,2,1,0:T(8,128)}, f32[4,2,8,1024]{3,2,1,0:T(8,128)S(1)}, u32[]{:S(2)}, u32[]{:S(2)}) collective-permute-start(f32[4,2,8,1024]{3,2,1,0:T(8,128)} %get-tuple-element.863), channel_id=1, source_target_pairs={{0,1},{1,2},{2,3},{4,5},{5,6},{6,7},{8,9},{9,10},{10,11},{12,13},{... | collective-permute-start | bytes 786440 | tf_op jit(solution)/shard_map/while/body/eval_jaxpr/ppermute | solution.py:22
  82.8 1.6 collective-permute-done.1
  84.7 2.6 fusion.117
  88.3 3.2 %fusion.118 = f32[2,72,1024]{2,1,0:T(8,128)S(1)} fusion(f32[2,2,72,1024]{3,2,1,0:T(8,128)S(1)} %fusion.117, f32[4,2,80,1024]{3,2,1,0:T(8,128)S(1)} %pad_maximum_fusion.23, s32[2,512]{1,0:T(2,128)S(1)} %copy-done.17, f32[72,1024]{1,0:T(8,128)S(1)} %bitcast.101, f32[72,1024]{1,0:T(8,128)S(1)} %bitcast.98, f32[2,512]{1,0:T(2,128)S(1)} %get-tuple-element.864, ...), kind=kOutput, calls=%fused_computation.109.clone.1 | convolution fusion | flops 909246464 | bytes 2961696 | tf_op jit(solution)/shard_map/while/body/eval_jaxpr/szr,srx->szx/dot_general | solution.py:84
  91.6 2.4 fusion.121
  95.2 3.1 %fusion.122 = f32[2,64,1024]{2,1,0:T(8,128)S(1)} fusion(s32[2,512]{1,0:T(2,128)S(1)} %copy-done.17, f32[2,2,64,1024]{3,2,1,0:T(8,128)S(1)} %fusion.121, f32[2,64,1024]{2,1,0:T(8,128)S(1)} %get-tuple-element.904, f32[2,64,1024]{2,1,0:T(8,128)S(1)} %get-tuple-element.927, f32[64,1024]{1,0:T(8,128)S(1)} %copy-done.12, ...), kind=kOutput, calls=%fused_computation.39.clone.1 | convolution fusion | flops 808452096 | bytes 2633984 | tf_op jit(solution)/shard_map/while/body/eval_jaxpr/szr,srx->szx/dot_general | solution.py:84
  101.4 4.9 %collective-permute-start.1 = (f32[4,2,8,1024]{3,2,1,0:T(8,128)}, f32[4,2,8,1024]{3,2,1,0:T(8,128)S(1)}, u32[]{:S(2)}, u32[]{:S(2)}) collective-permute-start(f32[4,2,8,1024]{3,2,1,0:T(8,128)} %get-tuple-element.863), channel_id=1, source_target_pairs={{0,1},{1,2},{2,3},{4,5},{5,6},{6,7},{8,9},{9,10},{10,11},{12,13},{... | collective-permute-start | bytes 786440 | tf_op jit(solution)/shard_map/while/body/eval_jaxpr/ppermute | solution.py:22
  110.8 2.6 fusion.117
  114.4 3.2 %fusion.118 = f32[2,72,1024]{2,1,0:T(8,128)S(1)} fusion(f32[2,2,72,1024]{3,2,1,0:T(8,128)S(1)} %fusion.117, f32[4,2,80,1024]{3,2,1,0:T(8,128)S(1)} %pad_maximum_fusion.23, s32[2,512]{1,0:T(2,128)S(1)} %copy-done.17, f32[72,1024]{1,0:T(8,128)S(1)} %bitcast.101, f32[72,1024]{1,0:T(8,128)S(1)} %bitcast.98, f32[2,512]{1,0:T(2,128)S(1)} %get-tuple-element.864, ...), kind=kOutput, calls=%fused_computation.109.clone.1 | convolution fusion | flops 909246464 | bytes 2961696 | tf_op jit(solution)/shard_map/while/body/eval_jaxpr/szr,srx->szx/dot_general | solution.py:84
  117.8 2.4 fusion.121
  121.4 3.1 %fusion.122 = f32[2,64,1024]{2,1,0:T(8,128)S(1)} fusion(s32[2,512]{1,0:T(2,128)S(1)} %copy-done.17, f32[2,2,64,1024]{3,2,1,0:T(8,128)S(1)} %fusion.121, f32[2,64,1024]{2,1,0:T(8,128)S(1)} %get-tuple-element.904, f32[2,64,1024]{2,1,0:T(8,128)S(1)} %get-tuple-element.927, f32[64,1024]{1,0:T(8,128)S(1)} %copy-done.12, ...), kind=kOutput, calls=%fused_computation.39.clone.1 | convolution fusion | flops 808452096 | bytes 2633984 | tf_op jit(solution)/shard_map/while/body/eval_jaxpr/szr,srx->szx/dot_general | solution.py:84
  127.6 4.9 %collective-permute-start.1 = (f32[4,2,8,1024]{3,2,1,0:T(8,128)}, f32[4,2,8,1024]{3,2,1,0:T(8,128)S(1)}, u32[]{:S(2)}, u32[]{:S(2)}) collective-permute-start(f32[4,2,8,1024]{3,2,1,0:T(8,128)} %get-tuple-element.863), channel_id=1, source_target_pairs={{0,1},{1,2},{2,3},{4,5},{5,6},{6,7},{8,9},{9,10},{10,11},{12,13},{... | collective-permute-start | bytes 786440 | tf_op jit(solution)/shard_map/while/body/eval_jaxpr/ppermute | solution.py:22
  137.0 2.6 fusion.117
  140.6 3.2 %fusion.118 = f32[2,72,1024]{2,1,0:T(8,128)S(1)} fusion(f32[2,2,72,1024]{3,2,1,0:T(8,128)S(1)} %fusion.117, f32[4,2,80,1024]{3,2,1,0:T(8,128)S(1)} %pad_maximum_fusion.23, s32[2,512]{1,0:T(2,128)S(1)} %copy-done.17, f32[72,1024]{1,0:T(8,128)S(1)} %bitcast.101, f32[72,1024]{1,0:T(8,128)S(1)} %bitcast.98, f32[2,512]{1,0:T(2,128)S(1)} %get-tuple-element.864, ...), kind=kOutput, calls=%fused_computation.109.clone.1 | convolution fusion | flops 909246464 | bytes 2961696 | tf_op jit(solution)/shard_map/while/body/eval_jaxpr/szr,srx->szx/dot_general | solution.py:84
  143.9 2.4 fusion.121
  147.6 3.1 %fusion.122 = f32[2,64,1024]{2,1,0:T(8,128)S(1)} fusion(s32[2,512]{1,0:T(2,128)S(1)} %copy-done.17, f32[2,2,64,1024]{3,2,1,0:T(8,128)S(1)} %fusion.121, f32[2,64,1024]{2,1,0:T(8,128)S(1)} %get-tuple-element.904, f32[2,64,1024]{2,1,0:T(8,128)S(1)} %get-tuple-element.927, f32[64,1024]{1,0:T(8,128)S(1)} %copy-done.12, ...), kind=kOutput, calls=%fused_computation.39.clone.1 | convolution fusion | flops 808452096 | bytes 2633984 | tf_op jit(solution)/shard_map/while/body/eval_jaxpr/szr,srx->szx/dot_general | solution.py:84
  153.7 4.9 %collective-permute-start.1 = (f32[4,2,8,1024]{3,2,1,0:T(8,128)}, f32[4,2,8,1024]{3,2,1,0:T(8,128)S(1)}, u32[]{:S(2)}, u32[]{:S(2)}) collective-permute-start(f32[4,2,8,1024]{3,2,1,0:T(8,128)} %get-tuple-element.863), channel_id=1, source_target_pairs={{0,1},{1,2},{2,3},{4,5},{5,6},{6,7},{8,9},{9,10},{10,11},{12,13},{... | collective-permute-start | bytes 786440 | tf_op jit(solution)/shard_map/while/body/eval_jaxpr/ppermute | solution.py:22
  163.2 2.6 fusion.117
  166.8 3.2 %fusion.118 = f32[2,72,1024]{2,1,0:T(8,128)S(1)} fusion(f32[2,2,72,1024]{3,2,1,0:T(8,128)S(1)} %fusion.117, f32[4,2,80,1024]{3,2,1,0:T(8,128)S(1)} %pad_maximum_fusion.23, s32[2,512]{1,0:T(2,128)S(1)} %copy-done.17, f32[72,1024]{1,0:T(8,128)S(1)} %bitcast.101, f32[72,1024]{1,0:T(8,128)S(1)} %bitcast.98, f32[2,512]{1,0:T(2,128)S(1)} %get-tuple-element.864, ...), kind=kOutput, calls=%fused_computation.109.clone.1 | convolution fusion | flops 909246464 | bytes 2961696 | tf_op jit(solution)/shard_map/while/body/eval_jaxpr/szr,srx->szx/dot_general | solution.py:84
  170.1 2.4 fusion.121
  173.8 3.1 %fusion.122 = f32[2,64,1024]{2,1,0:T(8,128)S(1)} fusion(s32[2,512]{1,0:T(2,128)S(1)} %copy-done.17, f32[2,2,64,1024]{3,2,1,0:T(8,128)S(1)} %fusion.121, f32[2,64,1024]{2,1,0:T(8,128)S(1)} %get-tuple-element.904, f32[2,64,1024]{2,1,0:T(8,128)S(1)} %get-tuple-element.927, f32[64,1024]{1,0:T(8,128)S(1)} %copy-done.12, ...), kind=kOutput, calls=%fused_computation.39.clone.1 | convolution fusion | flops 808452096 | bytes 2633984 | tf_op jit(solution)/shard_map/while/body/eval_jaxpr/szr,srx->szx/dot_general | solution.py:84
  179.9 4.9 %collective-permute-start.1 = (f32[4,2,8,1024]{3,2,1,0:T(8,128)}, f32[4,2,8,1024]{3,2,1,0:T(8,128)S(1)}, u32[]{:S(2)}, u32[]{:S(2)}) collective-permute-start(f32[4,2,8,1024]{3,2,1,0:T(8,128)} %get-tuple-element.863), channel_id=1, source_target_pairs={{0,1},{1,2},{2,3},{4,5},{5,6},{6,7},{8,9},{9,10},{10,11},{12,13},{... | collective-permute-start | bytes 786440 | tf_op jit(solution)/shard_map/while/body/eval_jaxpr/ppermute | solution.py:22
  187.4 1.6 collective-permute-done.1
  189.4 2.6 fusion.117
  193.0 3.2 %fusion.118 = f32[2,72,1024]{2,1,0:T(8,128)S(1)} fusion(f32[2,2,72,1024]{3,2,1,0:T(8,128)S(1)} %fusion.117, f32[4,2,80,1024]{3,2,1,0:T(8,128)S(1)} %pad_maximum_fusion.23, s32[2,512]{1,0:T(2,128)S(1)} %copy-done.17, f32[72,1024]{1,0:T(8,128)S(1)} %bitcast.101, f32[72,1024]{1,0:T(8,128)S(1)} %bitcast.98, f32[2,512]{1,0:T(2,128)S(1)} %get-tuple-element.864, ...), kind=kOutput, calls=%fused_computation.109.clone.1 | convolution fusion | flops 909246464 | bytes 2961696 | tf_op jit(solution)/shard_map/while/body/eval_jaxpr/szr,srx->szx/dot_general | solution.py:84
  196.3 2.4 fusion.121
  199.9 3.1 %fusion.122 = f32[2,64,1024]{2,1,0:T(8,128)S(1)} fusion(s32[2,512]{1,0:T(2,128)S(1)} %copy-done.17, f32[2,2,64,1024]{3,2,1,0:T(8,128)S(1)} %fusion.121, f32[2,64,1024]{2,1,0:T(8,128)S(1)} %get-tuple-element.904, f32[2,64,1024]{2,1,0:T(8,128)S(1)} %get-tuple-element.927, f32[64,1024]{1,0:T(8,128)S(1)} %copy-done.12, ...), kind=kOutput, calls=%fused_computation.39.clone.1 | convolution fusion | flops 808452096 | bytes 2633984 | tf_op jit(solution)/shard_map/while/body/eval_jaxpr/szr,srx->szx/dot_general | solution.py:84
  206.1 4.9 %collective-permute-start.1 = (f32[4,2,8,1024]{3,2,1,0:T(8,128)}, f32[4,2,8,1024]{3,2,1,0:T(8,128)S(1)}, u32[]{:S(2)}, u32[]{:S(2)}) collective-permute-start(f32[4,2,8,1024]{3,2,1,0:T(8,128)} %get-tuple-element.863), channel_id=1, source_target_pairs={{0,1},{1,2},{2,3},{4,5},{5,6},{6,7},{8,9},{9,10},{10,11},{12,13},{... | collective-permute-start | bytes 786440 | tf_op jit(solution)/shard_map/while/body/eval_jaxpr/ppermute | solution.py:22
  215.5 2.6 fusion.117
  219.1 3.2 %fusion.118 = f32[2,72,1024]{2,1,0:T(8,128)S(1)} fusion(f32[2,2,72,1024]{3,2,1,0:T(8,128)S(1)} %fusion.117, f32[4,2,80,1024]{3,2,1,0:T(8,128)S(1)} %pad_maximum_fusion.23, s32[2,512]{1,0:T(2,128)S(1)} %copy-done.17, f32[72,1024]{1,0:T(8,128)S(1)} %bitcast.101, f32[72,1024]{1,0:T(8,128)S(1)} %bitcast.98, f32[2,512]{1,0:T(2,128)S(1)} %get-tuple-element.864, ...), kind=kOutput, calls=%fused_computation.109.clone.1 | convolution fusion | flops 909246464 | bytes 2961696 | tf_op jit(solution)/shard_map/while/body/eval_jaxpr/szr,srx->szx/dot_general | solution.py:84
  222.4 2.4 fusion.121
  226.1 3.1 %fusion.122 = f32[2,64,1024]{2,1,0:T(8,128)S(1)} fusion(s32[2,512]{1,0:T(2,128)S(1)} %copy-done.17, f32[2,2,64,1024]{3,2,1,0:T(8,128)S(1)} %fusion.121, f32[2,64,1024]{2,1,0:T(8,128)S(1)} %get-tuple-element.904, f32[2,64,1024]{2,1,0:T(8,128)S(1)} %get-tuple-element.927, f32[64,1024]{1,0:T(8,128)S(1)} %copy-done.12, ...), kind=kOutput, calls=%fused_computation.39.clone.1 | convolution fusion | flops 808452096 | bytes 2633984 | tf_op jit(solution)/shard_map/while/body/eval_jaxpr/szr,srx->szx/dot_general | solution.py:84
  230.2 35.4 %all-reduce.4.cloned.1.call-done = f32[64,1024]{1,0:T(8,128)} async-done(((f32[64,1024]{1,0:T(8,128)}), f32[64,1024]{1,0:T(8,128)}) %all-reduce.4.cloned.1.call-update) | async-done | bytes 262160 | tf_op jit(solution)/shard_map/psum | solution.py:146
  265.6 1.7 broadcast_multiply_fusion
  (386 shorter events, 77.9 us)
Async XLA Ops:
  7.2 258.4 %all-reduce.4.cloned.1.call-start = ((), (), s32[]{:S(2)}) async-start(), calls=%async_computation | async-start | bytes 524288 | tf_op jit(solution)/shard_map/psum | solution.py:146
  7.2 1.7 copy-start.7
  7.2 8.2 %copy-start.13 = (f32[2,16,512]{2,1,0:T(8,128)S(1)}, f32[2,16,512]{2,1,0:T(8,128)}, u32[]{:S(2)}) copy-start(f32[2,16,512]{2,1,0:T(8,128)} %param.21) | copy-start | bytes 196612
  8.2 12.9 %copy-start.6 = (f32[2,64,1024]{2,1,0:T(8,128)S(1)}, f32[2,64,1024]{2,1,0:T(8,128)}, u32[]{:S(2)}) copy-start(f32[2,64,1024]{2,1,0:T(8,128)} %param.19) | copy-start | bytes 1572868
  8.9 12.1 %copy-start = (f32[256]{0:T(256)S(1)}, f32[256]{0:T(256)}, u32[]{:S(2)}) copy-start(f32[256]{0:T(256)} %param.22) | copy-start | bytes 3076
  8.9 12.1 %copy-start.1 = (f32[2,64,1024]{2,1,0:T(8,128)S(1)}, f32[2,64,1024]{2,1,0:T(8,128)}, u32[]{:S(2)}) copy-start(f32[2,64,1024]{2,1,0:T(8,128)} %param.17) | copy-start | bytes 1572868
  8.9 12.1 %copy-start.3 = (f32[2,64,1024]{2,1,0:T(8,128)S(1)}, f32[2,64,1024]{2,1,0:T(8,128)}, u32[]{:S(2)}) copy-start(f32[2,64,1024]{2,1,0:T(8,128)} %param.18) | copy-start | bytes 1572868
  8.9 12.1 %copy-start.5 = (f32[2,64,1024]{2,1,0:T(8,128)S(1)}, f32[2,64,1024]{2,1,0:T(8,128)}, u32[]{:S(2)}) copy-start(f32[2,64,1024]{2,1,0:T(8,128)} %param.20) | copy-start | bytes 1572868
  8.9 12.1 %copy-start.14 = (s32[2]{0:T(128)S(1)}, s32[2]{0:T(128)}, u32[]{:S(2)}) copy-start(s32[2]{0:T(128)} %param.27) | copy-start | bytes 28
  8.9 12.1 %copy-start.15 = (s32[2]{0:T(128)S(1)}, s32[2]{0:T(128)}, u32[]{:S(2)}) copy-start(s32[2]{0:T(128)} %param.24) | copy-start | bytes 28
  8.9 12.1 %copy-start.16 = (s32[2,512]{1,0:T(2,128)S(1)}, s32[2,512]{1,0:T(2,128)}, u32[]{:S(2)}) copy-start(s32[2,512]{1,0:T(2,128)} %param.25) | copy-start | bytes 12292
  9.0 12.1 %copy-start.18 = (s32[2]{0:T(128)S(1)}, s32[2]{0:T(128)}, u32[]{:S(2)}) copy-start(s32[2]{0:T(128)} %param.23) | copy-start | bytes 28
  9.0 7.0 %collective-permute-start.2 = (f32[2,8,1024]{2,1,0:T(8,128)S(1)}, f32[2,8,1024]{2,1,0:T(8,128)S(1)}, u32[]{:S(2)}, u32[]{:S(2)}) collective-permute-start(f32[2,8,1024]{2,1,0:T(8,128)S(1)} %get-tuple-element.729), channel_id=1, source_target_pairs={{0,1},{1,2},{2,3},{4,5},{5,6},{6,7},{8,9},{9,10},{10,11},{12,13},{... | collective-permute-start | bytes 196616 | tf_op jit(solution)/shard_map/ppermute | solution.py:22
  14.1 6.2 %collective-permute-start.3 = (f32[2,8,1024]{2,1,0:T(8,128)S(1)}, f32[2,8,1024]{2,1,0:T(8,128)S(1)}, u32[]{:S(2)}, u32[]{:S(2)}) collective-permute-start(f32[2,8,1024]{2,1,0:T(8,128)S(1)} %get-tuple-element.730), channel_id=1, source_target_pairs={{1,0},{2,1},{3,2},{5,4},{6,5},{7,6},{9,8},{10,9},{11,10},{13,12},{... | collective-permute-start | bytes 196616 | tf_op jit(solution)/shard_map/ppermute | solution.py:24
  21.9 8.7 %collective-permute-start = (f32[4,2,8,1024]{3,2,1,0:T(8,128)}, f32[4,2,8,1024]{3,2,1,0:T(8,128)S(1)}, u32[]{:S(2)}, u32[]{:S(2)}) collective-permute-start(f32[4,2,8,1024]{3,2,1,0:T(8,128)} %get-tuple-element.862), channel_id=1, source_target_pairs={{1,0},{2,1},{3,2},{5,4},{6,5},{7,6},{9,8},{10,9},{11,10},{13,12},{... | collective-permute-start | bytes 786440 | tf_op jit(solution)/shard_map/while/body/eval_jaxpr/ppermute | solution.py:24
  23.2 8.7 %collective-permute-start.1 = (f32[4,2,8,1024]{3,2,1,0:T(8,128)}, f32[4,2,8,1024]{3,2,1,0:T(8,128)S(1)}, u32[]{:S(2)}, u32[]{:S(2)}) collective-permute-start(f32[4,2,8,1024]{3,2,1,0:T(8,128)} %get-tuple-element.863), channel_id=1, source_target_pairs={{0,1},{1,2},{2,3},{4,5},{5,6},{6,7},{8,9},{9,10},{10,11},{12,13},{... | collective-permute-start | bytes 786440 | tf_op jit(solution)/shard_map/while/body/eval_jaxpr/ppermute | solution.py:22
  42.9 3.1 %copy-start.8 = (f32[64,1024]{1,0:T(8,128)S(1)}, f32[64,1024]{1,0:T(8,128)}, u32[]{:S(2)}) copy-start(f32[64,1024]{1,0:T(8,128)} %get-tuple-element.905) | copy-start | bytes 786436 | tf_op jit(solution)/shard_map/while
  42.9 4.0 %copy-start.19 = (s32[2]{0:T(128)S(1)}, s32[2]{0:T(128)}, u32[]{:S(2)}) copy-start(s32[2]{0:T(128)} %get-tuple-element.982) | copy-start | bytes 28 | tf_op jit(solution)/shard_map/while
  47.8 8.8 %collective-permute-start = (f32[4,2,8,1024]{3,2,1,0:T(8,128)}, f32[4,2,8,1024]{3,2,1,0:T(8,128)S(1)}, u32[]{:S(2)}, u32[]{:S(2)}) collective-permute-start(f32[4,2,8,1024]{3,2,1,0:T(8,128)} %get-tuple-element.862), channel_id=1, source_target_pairs={{1,0},{2,1},{3,2},{5,4},{6,5},{7,6},{9,8},{10,9},{11,10},{13,12},{... | collective-permute-start | bytes 786440 | tf_op jit(solution)/shard_map/while/body/eval_jaxpr/ppermute | solution.py:24
  49.0 9.1 %collective-permute-start.1 = (f32[4,2,8,1024]{3,2,1,0:T(8,128)}, f32[4,2,8,1024]{3,2,1,0:T(8,128)S(1)}, u32[]{:S(2)}, u32[]{:S(2)}) collective-permute-start(f32[4,2,8,1024]{3,2,1,0:T(8,128)} %get-tuple-element.863), channel_id=1, source_target_pairs={{0,1},{1,2},{2,3},{4,5},{5,6},{6,7},{8,9},{9,10},{10,11},{12,13},{... | collective-permute-start | bytes 786440 | tf_op jit(solution)/shard_map/while/body/eval_jaxpr/ppermute | solution.py:22
  69.1 3.1 %copy-start.8 = (f32[64,1024]{1,0:T(8,128)S(1)}, f32[64,1024]{1,0:T(8,128)}, u32[]{:S(2)}) copy-start(f32[64,1024]{1,0:T(8,128)} %get-tuple-element.905) | copy-start | bytes 786436 | tf_op jit(solution)/shard_map/while
  69.1 4.0 %copy-start.19 = (s32[2]{0:T(128)S(1)}, s32[2]{0:T(128)}, u32[]{:S(2)}) copy-start(s32[2]{0:T(128)} %get-tuple-element.982) | copy-start | bytes 28 | tf_op jit(solution)/shard_map/while
  73.9 8.8 %collective-permute-start = (f32[4,2,8,1024]{3,2,1,0:T(8,128)}, f32[4,2,8,1024]{3,2,1,0:T(8,128)S(1)}, u32[]{:S(2)}, u32[]{:S(2)}) collective-permute-start(f32[4,2,8,1024]{3,2,1,0:T(8,128)} %get-tuple-element.862), channel_id=1, source_target_pairs={{1,0},{2,1},{3,2},{5,4},{6,5},{7,6},{9,8},{10,9},{11,10},{13,12},{... | collective-permute-start | bytes 786440 | tf_op jit(solution)/shard_map/while/body/eval_jaxpr/ppermute | solution.py:24
  75.2 9.1 %collective-permute-start.1 = (f32[4,2,8,1024]{3,2,1,0:T(8,128)}, f32[4,2,8,1024]{3,2,1,0:T(8,128)S(1)}, u32[]{:S(2)}, u32[]{:S(2)}) collective-permute-start(f32[4,2,8,1024]{3,2,1,0:T(8,128)} %get-tuple-element.863), channel_id=1, source_target_pairs={{0,1},{1,2},{2,3},{4,5},{5,6},{6,7},{8,9},{9,10},{10,11},{12,13},{... | collective-permute-start | bytes 786440 | tf_op jit(solution)/shard_map/while/body/eval_jaxpr/ppermute | solution.py:22
  95.2 3.1 %copy-start.8 = (f32[64,1024]{1,0:T(8,128)S(1)}, f32[64,1024]{1,0:T(8,128)}, u32[]{:S(2)}) copy-start(f32[64,1024]{1,0:T(8,128)} %get-tuple-element.905) | copy-start | bytes 786436 | tf_op jit(solution)/shard_map/while
  95.2 4.0 %copy-start.19 = (s32[2]{0:T(128)S(1)}, s32[2]{0:T(128)}, u32[]{:S(2)}) copy-start(s32[2]{0:T(128)} %get-tuple-element.982) | copy-start | bytes 28 | tf_op jit(solution)/shard_map/while
  100.1 8.8 %collective-permute-start = (f32[4,2,8,1024]{3,2,1,0:T(8,128)}, f32[4,2,8,1024]{3,2,1,0:T(8,128)S(1)}, u32[]{:S(2)}, u32[]{:S(2)}) collective-permute-start(f32[4,2,8,1024]{3,2,1,0:T(8,128)} %get-tuple-element.862), channel_id=1, source_target_pairs={{1,0},{2,1},{3,2},{5,4},{6,5},{7,6},{9,8},{10,9},{11,10},{13,12},{... | collective-permute-start | bytes 786440 | tf_op jit(solution)/shard_map/while/body/eval_jaxpr/ppermute | solution.py:24
  101.4 9.1 %collective-permute-start.1 = (f32[4,2,8,1024]{3,2,1,0:T(8,128)}, f32[4,2,8,1024]{3,2,1,0:T(8,128)S(1)}, u32[]{:S(2)}, u32[]{:S(2)}) collective-permute-start(f32[4,2,8,1024]{3,2,1,0:T(8,128)} %get-tuple-element.863), channel_id=1, source_target_pairs={{0,1},{1,2},{2,3},{4,5},{5,6},{6,7},{8,9},{9,10},{10,11},{12,13},{... | collective-permute-start | bytes 786440 | tf_op jit(solution)/shard_map/while/body/eval_jaxpr/ppermute | solution.py:22
  121.4 3.1 %copy-start.8 = (f32[64,1024]{1,0:T(8,128)S(1)}, f32[64,1024]{1,0:T(8,128)}, u32[]{:S(2)}) copy-start(f32[64,1024]{1,0:T(8,128)} %get-tuple-element.905) | copy-start | bytes 786436 | tf_op jit(solution)/shard_map/while
  121.4 4.0 %copy-start.19 = (s32[2]{0:T(128)S(1)}, s32[2]{0:T(128)}, u32[]{:S(2)}) copy-start(s32[2]{0:T(128)} %get-tuple-element.982) | copy-start | bytes 28 | tf_op jit(solution)/shard_map/while
  126.3 8.8 %collective-permute-start = (f32[4,2,8,1024]{3,2,1,0:T(8,128)}, f32[4,2,8,1024]{3,2,1,0:T(8,128)S(1)}, u32[]{:S(2)}, u32[]{:S(2)}) collective-permute-start(f32[4,2,8,1024]{3,2,1,0:T(8,128)} %get-tuple-element.862), channel_id=1, source_target_pairs={{1,0},{2,1},{3,2},{5,4},{6,5},{7,6},{9,8},{10,9},{11,10},{13,12},{... | collective-permute-start | bytes 786440 | tf_op jit(solution)/shard_map/while/body/eval_jaxpr/ppermute | solution.py:24
  127.6 9.1 %collective-permute-start.1 = (f32[4,2,8,1024]{3,2,1,0:T(8,128)}, f32[4,2,8,1024]{3,2,1,0:T(8,128)S(1)}, u32[]{:S(2)}, u32[]{:S(2)}) collective-permute-start(f32[4,2,8,1024]{3,2,1,0:T(8,128)} %get-tuple-element.863), channel_id=1, source_target_pairs={{0,1},{1,2},{2,3},{4,5},{5,6},{6,7},{8,9},{9,10},{10,11},{12,13},{... | collective-permute-start | bytes 786440 | tf_op jit(solution)/shard_map/while/body/eval_jaxpr/ppermute | solution.py:22
  147.6 3.1 %copy-start.8 = (f32[64,1024]{1,0:T(8,128)S(1)}, f32[64,1024]{1,0:T(8,128)}, u32[]{:S(2)}) copy-start(f32[64,1024]{1,0:T(8,128)} %get-tuple-element.905) | copy-start | bytes 786436 | tf_op jit(solution)/shard_map/while
  147.6 4.0 %copy-start.19 = (s32[2]{0:T(128)S(1)}, s32[2]{0:T(128)}, u32[]{:S(2)}) copy-start(s32[2]{0:T(128)} %get-tuple-element.982) | copy-start | bytes 28 | tf_op jit(solution)/shard_map/while
  152.4 8.8 %collective-permute-start = (f32[4,2,8,1024]{3,2,1,0:T(8,128)}, f32[4,2,8,1024]{3,2,1,0:T(8,128)S(1)}, u32[]{:S(2)}, u32[]{:S(2)}) collective-permute-start(f32[4,2,8,1024]{3,2,1,0:T(8,128)} %get-tuple-element.862), channel_id=1, source_target_pairs={{1,0},{2,1},{3,2},{5,4},{6,5},{7,6},{9,8},{10,9},{11,10},{13,12},{... | collective-permute-start | bytes 786440 | tf_op jit(solution)/shard_map/while/body/eval_jaxpr/ppermute | solution.py:24
  153.7 9.1 %collective-permute-start.1 = (f32[4,2,8,1024]{3,2,1,0:T(8,128)}, f32[4,2,8,1024]{3,2,1,0:T(8,128)S(1)}, u32[]{:S(2)}, u32[]{:S(2)}) collective-permute-start(f32[4,2,8,1024]{3,2,1,0:T(8,128)} %get-tuple-element.863), channel_id=1, source_target_pairs={{0,1},{1,2},{2,3},{4,5},{5,6},{6,7},{8,9},{9,10},{10,11},{12,13},{... | collective-permute-start | bytes 786440 | tf_op jit(solution)/shard_map/while/body/eval_jaxpr/ppermute | solution.py:22
  173.8 3.1 %copy-start.8 = (f32[64,1024]{1,0:T(8,128)S(1)}, f32[64,1024]{1,0:T(8,128)}, u32[]{:S(2)}) copy-start(f32[64,1024]{1,0:T(8,128)} %get-tuple-element.905) | copy-start | bytes 786436 | tf_op jit(solution)/shard_map/while
  173.8 4.0 %copy-start.19 = (s32[2]{0:T(128)S(1)}, s32[2]{0:T(128)}, u32[]{:S(2)}) copy-start(s32[2]{0:T(128)} %get-tuple-element.982) | copy-start | bytes 28 | tf_op jit(solution)/shard_map/while
  178.6 8.8 %collective-permute-start = (f32[4,2,8,1024]{3,2,1,0:T(8,128)}, f32[4,2,8,1024]{3,2,1,0:T(8,128)S(1)}, u32[]{:S(2)}, u32[]{:S(2)}) collective-permute-start(f32[4,2,8,1024]{3,2,1,0:T(8,128)} %get-tuple-element.862), channel_id=1, source_target_pairs={{1,0},{2,1},{3,2},{5,4},{6,5},{7,6},{9,8},{10,9},{11,10},{13,12},{... | collective-permute-start | bytes 786440 | tf_op jit(solution)/shard_map/while/body/eval_jaxpr/ppermute | solution.py:24
  179.9 9.1 %collective-permute-start.1 = (f32[4,2,8,1024]{3,2,1,0:T(8,128)}, f32[4,2,8,1024]{3,2,1,0:T(8,128)S(1)}, u32[]{:S(2)}, u32[]{:S(2)}) collective-permute-start(f32[4,2,8,1024]{3,2,1,0:T(8,128)} %get-tuple-element.863), channel_id=1, source_target_pairs={{0,1},{1,2},{2,3},{4,5},{5,6},{6,7},{8,9},{9,10},{10,11},{12,13},{... | collective-permute-start | bytes 786440 | tf_op jit(solution)/shard_map/while/body/eval_jaxpr/ppermute | solution.py:22
  199.9 3.1 %copy-start.8 = (f32[64,1024]{1,0:T(8,128)S(1)}, f32[64,1024]{1,0:T(8,128)}, u32[]{:S(2)}) copy-start(f32[64,1024]{1,0:T(8,128)} %get-tuple-element.905) | copy-start | bytes 786436 | tf_op jit(solution)/shard_map/while
  199.9 4.0 %copy-start.19 = (s32[2]{0:T(128)S(1)}, s32[2]{0:T(128)}, u32[]{:S(2)}) copy-start(s32[2]{0:T(128)} %get-tuple-element.982) | copy-start | bytes 28 | tf_op jit(solution)/shard_map/while
  204.8 8.8 %collective-permute-start = (f32[4,2,8,1024]{3,2,1,0:T(8,128)}, f32[4,2,8,1024]{3,2,1,0:T(8,128)S(1)}, u32[]{:S(2)}, u32[]{:S(2)}) collective-permute-start(f32[4,2,8,1024]{3,2,1,0:T(8,128)} %get-tuple-element.862), channel_id=1, source_target_pairs={{1,0},{2,1},{3,2},{5,4},{6,5},{7,6},{9,8},{10,9},{11,10},{13,12},{... | collective-permute-start | bytes 786440 | tf_op jit(solution)/shard_map/while/body/eval_jaxpr/ppermute | solution.py:24
  206.1 9.1 %collective-permute-start.1 = (f32[4,2,8,1024]{3,2,1,0:T(8,128)}, f32[4,2,8,1024]{3,2,1,0:T(8,128)S(1)}, u32[]{:S(2)}, u32[]{:S(2)}) collective-permute-start(f32[4,2,8,1024]{3,2,1,0:T(8,128)} %get-tuple-element.863), channel_id=1, source_target_pairs={{0,1},{1,2},{2,3},{4,5},{5,6},{6,7},{8,9},{9,10},{10,11},{12,13},{... | collective-permute-start | bytes 786440 | tf_op jit(solution)/shard_map/while/body/eval_jaxpr/ppermute | solution.py:22
  226.1 3.1 %copy-start.8 = (f32[64,1024]{1,0:T(8,128)S(1)}, f32[64,1024]{1,0:T(8,128)}, u32[]{:S(2)}) copy-start(f32[64,1024]{1,0:T(8,128)} %get-tuple-element.905) | copy-start | bytes 786436 | tf_op jit(solution)/shard_map/while
  226.1 4.0 %copy-start.19 = (s32[2]{0:T(128)S(1)}, s32[2]{0:T(128)}, u32[]{:S(2)}) copy-start(s32[2]{0:T(128)} %get-tuple-element.982) | copy-start | bytes 28 | tf_op jit(solution)/shard_map/while
  230.1 37.1 %copy-start.2 = (f32[2,64,1024]{2,1,0:T(8,128)}, f32[2,64,1024]{2,1,0:T(8,128)S(1)}, u32[]{:S(2)}) copy-start(f32[2,64,1024]{2,1,0:T(8,128)S(1)} %get-tuple-element.960) | copy-start | bytes 1572868
  230.1 37.1 %copy-start.4 = (f32[2,64,1024]{2,1,0:T(8,128)}, f32[2,64,1024]{2,1,0:T(8,128)S(1)}, u32[]{:S(2)}) copy-start(f32[2,64,1024]{2,1,0:T(8,128)S(1)} %get-tuple-element.962) | copy-start | bytes 1572868
  (65 other events, 53.8 us)
Sparse Core Ops, SparseCore 0:
  230.3 35.2 all-reduce.3
where the time goes:
time: 275 us; the launch traced here: 274 us
  other arithmetic  63.9 us (23%)
  waiting for transfers between devices  56.8 us (21%)
  starting transfers between devices  55.7 us (20%)
  matrix products  50.3 us (18%)
  local copies, waits for them, and re-layouts  31.5 us (11%)
  between operations  14.2 us (5%)
    dot_general x16, matrix products, advance(): jnp.einsum('szr,srx->szx', depth_table, lateral_table, precision=lax.Prec...  50.3 us
    ppermute x9, starting transfers between devices, extended_2(): lax.ppermute(tail, axis, [(i, (i + 1) % count) for i in range(ends)])  44.1 us
    add x16, other arithmetic, laplace(): result + stencil_coeffs[offset] * (extended[..., 4 + offset:4 + offset +...  39.8 us
    psum x1, waiting for transfers between devices, local(): image_total = lax.psum(carry[4], 'shot')  35.4 us
    while x160, local copies, waits for them, and re-layouts  18.2 us
    ppermute x9, waiting for transfers between devices, extended_2(): lax.ppermute(tail, axis, [(i, (i + 1) % count) for i in range(ends)])  12.8 us
    ppermute x9, starting transfers between devices, extended_2(): lax.ppermute(head, axis, [((i + 1) % count, i) for i in range(ends)])  11.5 us
    gather x16, local copies, waits for them, and re-layouts, advance(): pulse = wavelet[checkpoint_step + STEPS - 1 - step_index]  10.2 us
  transfers between devices with their start and end apart: 19, of which 19 were waited for; matrix products, arithmetic and copies ran while one was open for 5% of the time, Pallas kernels for 0%

commit v1 on v0

v1 whole, which is shorter than its diff:
```python
import functools
import math

import jax
import jax.numpy as jnp
from jax import lax
from jax.experimental import pallas as pl
from jax.experimental.pallas import tpu as pltpu
from jax.sharding import PartitionSpec as P

STEPS = 16
PAIRS = STEPS // 2
MESH = pl.DeviceIdType.MESH
LANES = 128
HALO = 8

coeffs = (-205.0 / 72.0, 8.0 / 5.0, -1.0 / 5.0, 8.0 / 315.0, -1.0 / 560.0)


def kernel(
    slabs,
    shot_devices,
    scale,
    wavelet,
    checkpoint,
    s_depth,
    s_lateral,
    velocity_in,
    sponge_in,
    s_later,
    s_now,
    r_later,
    r_now,
    traces,
    r_depth,
    table,
    image_out,
    s_out,
    r_out,
    even,
    odd,
    velocity,
    damping,
    source,
    corr,
    inject_1,
    inject_2,
    slots,
    start_fields,
    start_velocity,
    start_sponge,
    pair_buf,
    chip_src,
    chip_buf,
    last_src,
    last_buf,
    send_sem,
    recv_sem,
    start_send,
    start_recv,
    sum_send,
    sum_recv,
):
    shots, rows, width = s_now.shape
    blocks = width // LANES
    me = lax.axis_index("slab")
    shot_me = lax.axis_index("shot")
    has_up = me > 0
    has_down = me < slabs - 1
    up = jnp.maximum(me - 1, 0)
    down = jnp.minimum(me + 1, slabs - 1)
    first_row = me * rows
    lane = lax.broadcasted_iota(jnp.int32, (8, LANES), 1)
    sub = lax.broadcasted_iota(jnp.int32, (8, LANES), 0)
    zero = jnp.zeros((8, LANES), jnp.float32)

    barrier = pltpu.get_barrier_semaphore()

    @pl.when(has_up)
    def _():
        pl.semaphore_signal(barrier, inc=1, device_id={"slab": up}, device_id_type=MESH)

    @pl.when(has_down)
    def _():
        pl.semaphore_signal(barrier, inc=1, device_id={"slab": down}, device_id_type=MESH)

    for other in range(1, shot_devices):
        target = lax.rem(shot_me + other, shot_devices)
        pl.semaphore_signal(barrier, inc=1, device_id={"shot": target}, device_id_type=MESH)
    pl.semaphore_wait(
        barrier, shot_devices - 1 + has_up.astype(jnp.int32) + has_down.astype(jnp.int32)
    )

    def start_copies(side):
        first = 0 if side == 1 else rows - HALO
        target = up if side == 1 else down
        copies = []
        sources = [
            (s_now.at[:, pl.ds(first, HALO), :], start_fields.at[side, 0]),
            (s_later.at[:, pl.ds(first, HALO), :], start_fields.at[side, 1]),
            (velocity_in.at[pl.ds(first, HALO), :], start_velocity.at[side]),
            (r_now.at[:, pl.ds(first, HALO), :], start_fields.at[side, 2]),
            (r_later.at[:, pl.ds(first, HALO), :], start_fields.at[side, 3]),
            (sponge_in.at[pl.ds(first, HALO), :], start_sponge.at[side]),
        ]
        for number, (src, dst) in enumerate(sources):
            copies.append(
                pltpu.make_async_remote_copy(
                    src_ref=src,
                    dst_ref=dst,
                    send_sem=start_send.at[side, number],
                    recv_sem=start_recv.at[side, number],
                    device_id={"slab": target},
                    device_id_type=MESH,
                )
            )
        return copies

    @pl.when(has_up)
    def _():
        for copy in start_copies(1):
            copy.start()

    @pl.when(has_down)
    def _():
        for copy in start_copies(0):
            copy.start()

    def put_rows(row, side_now, side_later, velocity_rows, sponge_rows):
        for j in range(blocks):
            cut = pl.ds(j * LANES, LANES)
            speed = velocity_rows(cut)
            velocity[j, pl.ds(row, 8), :] = speed
            damping[j, pl.ds(row, 8), :] = 1.0 - 0.06 * sponge_rows(cut).astype(jnp.float32)
            row_ids = first_row - HALO + row + sub
            column_ids = j * LANES + lane
            for s in range(shots):
                hit = (row_ids == s_depth[s]) & (column_ids == s_lateral[s])
                source[s, j, pl.ds(row, 8), :] = jnp.where(hit, -speed, 0.0)
                for f in range(2):
                    even[2 * s + f, j, pl.ds(row, 8), :] = side_now(f, s, cut)
                    odd[2 * s + f, j, pl.ds(row, 8), :] = side_later(f, s, cut)

    for tile in range(rows // 8):
        r = tile * 8
        put_rows(
            HALO + r,
            lambda f, s, cut: (s_now, r_now)[f][s, pl.ds(r, 8), cut],
            lambda f, s, cut: (s_later, r_later)[f][s, pl.ds(r, 8), cut],
            lambda cut: velocity_in[pl.ds(r, 8), cut],
            lambda cut: sponge_in[pl.ds(r, 8), cut],
        )
        for j in range(blocks):
            cut = pl.ds(j * LANES, LANES)
            total = s_now[0, pl.ds(r, 8), cut] * r_now[0, pl.ds(r, 8), cut]
            for s in range(1, shots):
                total = total + s_now[s, pl.ds(r, 8), cut] * r_now[s, pl.ds(r, 8), cut]
            corr[j, pl.ds(r, 8), :] = total

    for side, present, row in ((0, has_up, 0), (1, has_down, HALO + rows)):

        @pl.when(present)
        def _():
            for copy in start_copies(1 - side):
                copy.wait_send()
            for copy in start_copies(side):
                copy.wait_recv()
            put_rows(
                row,
                lambda f, s, cut: start_fields[side, 2 * f, s, :, cut],
                lambda f, s, cut: start_fields[side, 2 * f + 1, s, :, cut],
                lambda cut: start_velocity[side, :, cut],
                lambda cut: start_sponge[side, :, cut],
            )

        @pl.when(jnp.logical_not(present))
        def _():
            for j in range(blocks):
                velocity[j, pl.ds(row, 8), :] = zero
                damping[j, pl.ds(row, 8), :] = zero
                for s in range(shots):
                    source[s, j, pl.ds(row, 8), :] = zero
                    for f in range(2):
                        even[2 * s + f, j, pl.ds(row, 8), :] = zero
                        odd[2 * s + f, j, pl.ds(row, 8), :] = zero

    def laplace_rows(ref, w, row, j, centre):
        total = (2.0 * coeffs[0]) * centre[j]
        left = centre[j - 1] if j > 0 else zero
        right = centre[j + 1] if j < blocks - 1 else zero
        for k in range(1, 5):
            ahead = pltpu.roll(jnp.where(lane >= k, centre[j], right), LANES - k, 1)
            behind = pltpu.roll(jnp.where(lane < LANES - k, centre[j], left), k, 1)
            total = total + coeffs[k] * (
                (ref[w, j, pl.ds(row + k, 8), :] + ref[w, j, pl.ds(row - k, 8), :])
                + (ahead + behind)
            )
        return total

    def source_tile(now, later, s, row, pulse):
        w = 2 * s
        centre = [now[w, j, pl.ds(row, 8), :] for j in range(blocks)]
        for j in range(blocks):
            lap = laplace_rows(now, w, row, j, centre)
            later[w, j, pl.ds(row, 8), :] = (
                (centre[j] + centre[j] - later[w, j, pl.ds(row, 8), :])
                + velocity[j, pl.ds(row, 8), :] * lap
                + pulse * source[s, j, pl.ds(row, 8), :]
            )

    def receiver_tile(now, later, s, row, inject, inject_row):
        w = 2 * s + 1
        centre = [now[w, j, pl.ds(row, 8), :] for j in range(blocks)]
        for j in range(blocks):
            lap = laplace_rows(now, w, row, j, centre)
            lap = lap + inject[pl.ds(inject_row, 8), pl.ds(j * LANES, LANES)]
            later[w, j, pl.ds(row, 8), :] = damping[j, pl.ds(row, 8), :] * (
                (centre[j] + centre[j] - later[w, j, pl.ds(row, 8), :])
                + velocity[j, pl.ds(row, 8), :] * lap
            )

    def halo_copy(w, parity, side):
        first = HALO if side == 1 else rows
        target = up if side == 1 else down
        return pltpu.make_async_remote_copy(
            src_ref=even.at[w, :, pl.ds(first, HALO), :],
            dst_ref=slots.at[parity, side, w],
            send_sem=send_sem.at[parity, side, w],
            recv_sem=recv_sem.at[parity, side, w],
            device_id={"slab": target},
            device_id_type=MESH,
        )

    tiles = rows // 8

    def one_field(pair, s, f, step_1, step_2):
        w = 2 * s + f
        sent = lax.rem(pair + 1, 2)
        slot = lax.rem(pair, 2)
        for t in range(1, tiles):
            step_1(4 + 8 * t, 8 * t)
        for side, present, row in ((0, has_up, 0), (1, has_down, HALO + rows)):

            @pl.when(present & (pair > 0))
            def _():
                halo_copy(w, sent, 1 - side).wait_send()
                halo_copy(w, sent, side).wait_recv()
                for j in range(blocks):
                    even[w, j, pl.ds(row, 8), :] = slots[sent, side, w, j]

        step_1(4, 0)
        step_1(4 + rows, rows)
        step_2(HALO, 0)
        step_2(HALO + rows - 8, rows - 8)
        for side, present in ((1, has_up), (0, has_down)):

            @pl.when(present & (pair < PAIRS - 1))
            def _():
                halo_copy(w, slot, side).start()

        for t in range(1, tiles - 1):
            step_2(HALO + 8 * t, 8 * t)

    def injection(pair, s):
        ids = first_row + lax.broadcasted_iota(jnp.int32, (rows + 8, r_depth.shape[1]), 0)
        depth = r_depth[pl.ds(s, 1), :]
        hit_1 = (ids - 4) == depth
        hit_2 = ids[:rows] == depth
        parts = []
        for hit, step in ((hit_1, 2 * pair), (hit_2, 2 * pair + 1)):
            trace = traces[s, pl.ds(step, 1), :]
            high = trace.astype(jnp.bfloat16).astype(jnp.float32)
            parts.append(jnp.where(hit, high, 0.0))
            parts.append(jnp.where(hit, trace - high, 0.0))
        stacked = jnp.concatenate(parts, axis=0).astype(jnp.bfloat16)
        wide = 2 * LANES
        one = rows + 8
        for n in range(width // wide):
            cut = pl.ds(n * wide, wide)
            out = jnp.dot(stacked, table[s, :, cut], preferred_element_type=jnp.float32)
            inject_1[:, cut] = out[:one] + out[one : 2 * one]
            inject_2[:, cut] = out[2 * one : 2 * one + rows] + out[2 * one + rows :]

    def shot_pair(pair, s):
        step = checkpoint[s] + STEPS - 1 - 2 * pair
        pulse_1 = wavelet[step]
        pulse_2 = wavelet[step - 1]

        @pl.when(pair > 0)
        def _():
            for t in range(tiles):
                for j in range(blocks):
                    cut = pl.ds(HALO + 8 * t, 8)
                    corr[j, pl.ds(8 * t, 8), :] += even[2 * s, j, cut, :] * even[2 * s + 1, j, cut, :]

        one_field(
            pair,
            s,
            0,
            lambda row, _: source_tile(even, odd, s, row, pulse_1),
            lambda row, _: source_tile(odd, even, s, row, pulse_2),
        )
        injection(pair, s)
        one_field(
            pair,
            s,
            1,
            lambda row, at: receiver_tile(even, odd, s, row, inject_1, at),
            lambda row, at: receiver_tile(odd, even, s, row, inject_2, at),
        )
        for t in range(tiles):
            for j in range(blocks):
                cut = pl.ds(HALO + 8 * t, 8)
                corr[j, pl.ds(8 * t, 8), :] += odd[2 * s, j, cut, :] * odd[2 * s + 1, j, cut, :]

    def turn(index, carry):
        shot_pair(index // shots, lax.rem(index, shots))
        return carry

    lax.fori_loop(0, PAIRS * shots, turn, 0)

    half = rows // 2
    odd_one = lax.rem(shot_me, 2)
    mate = shot_me + 1 - 2 * odd_one
    keep = pl.multiple_of(odd_one * half, 8)
    give = pl.multiple_of((1 - odd_one) * half, 8)
    chips = shot_devices // 2
    first = pltpu.make_async_remote_copy(
        src_ref=corr.at[:, pl.ds(give, half), :],
        dst_ref=pair_buf,
        send_sem=sum_send.at[0],
        recv_sem=sum_recv.at[0],
        device_id={"shot": mate},
        device_id_type=MESH,
    )
    first.start()
    for t in range(rows // 8):
        for j in range(blocks):
            for s in range(shots):
                cut = pl.ds(HALO + 8 * t, 8)
                s_out[s, pl.ds(8 * t, 8), pl.ds(j * LANES, LANES)] = even[2 * s, j, cut, :]
                r_out[s, pl.ds(8 * t, 8), pl.ds(j * LANES, LANES)] = even[2 * s + 1, j, cut, :]
    first.wait()
    chip_src[...] = corr[:, pl.ds(keep, half), :] + pair_buf[...]
    others = []
    for other in range(1, chips):
        target = lax.rem(shot_me + 2 * other, shot_devices)
        copy = pltpu.make_async_remote_copy(
            src_ref=chip_src,
            dst_ref=chip_buf.at[other - 1],
            send_sem=sum_send.at[1 + other],
            recv_sem=sum_recv.at[1 + other],
            device_id={"shot": target},
            device_id_type=MESH,
        )
        copy.start()
        others.append(copy)
    total = chip_src[...]
    for number, copy in enumerate(others):
        copy.wait()
        total = total + chip_buf[number]
    last_src[...] = total * scale
    last = pltpu.make_async_remote_copy(
        src_ref=last_src,
        dst_ref=last_buf,
        send_sem=sum_send.at[1],
        recv_sem=sum_recv.at[1],
        device_id={"shot": mate},
        device_id_type=MESH,
    )
    last.start()
    for j in range(blocks):
        image_out[pl.ds(keep, half), pl.ds(j * LANES, LANES)] = last_src[j]
    last.wait()
    for j in range(blocks):
        image_out[pl.ds(give, half), pl.ds(j * LANES, LANES)] = last_buf[j]


def local(slabs, shot_devices, courant_sq, sponge_level, source_later, source_now, receiver_later,
          receiver_now, traces, wavelet, source_depth, source_lateral, receiver_depth,
          receiver_lateral, checkpoint_step):
    shots, rows, width = source_now.shape
    blocks = width // LANES
    wide = rows + 2 * HALO
    lateral_ids = jnp.arange(width, dtype=jnp.int32)
    table = (receiver_lateral[:, :, None] == lateral_ids[None, None, :]).astype(jnp.bfloat16)
    vmem = pl.BlockSpec(memory_space=pltpu.VMEM)
    smem = pl.BlockSpec(memory_space=pltpu.SMEM)
    f32 = jnp.float32
    half = rows // 2
    chips = shot_devices // 2
    return pl.pallas_call(
        functools.partial(kernel, slabs, shot_devices, 1.0 / math.sqrt(STEPS * shots * shot_devices)),
        out_shape=(
            jax.ShapeDtypeStruct((rows, width), f32),
            jax.ShapeDtypeStruct((shots, rows, width), f32),
            jax.ShapeDtypeStruct((shots, rows, width), f32),
        ),
        in_specs=[smem] * 4 + [vmem] * 9,
        out_specs=(vmem, vmem, vmem),
        scratch_shapes=[
            pltpu.VMEM((2 * shots, blocks, wide, LANES), f32),
            pltpu.VMEM((2 * shots, blocks, wide, LANES), f32),
            pltpu.VMEM((blocks, wide, LANES), f32),
            pltpu.VMEM((blocks, wide, LANES), f32),
            pltpu.VMEM((shots, blocks, wide, LANES), f32),
            pltpu.VMEM((blocks, rows, LANES), f32),
            pltpu.VMEM((rows + 8, width), f32),
            pltpu.VMEM((rows, width), f32),
            pltpu.VMEM((2, 2, 2 * shots, blocks, HALO, LANES), f32),
            pltpu.VMEM((2, 4, shots, HALO, width), f32),
            pltpu.VMEM((2, HALO, width), f32),
            pltpu.VMEM((2, HALO, width), jnp.int32),
            pltpu.VMEM((blocks, half, LANES), f32),
            pltpu.VMEM((blocks, half, LANES), f32),
            pltpu.VMEM((max(chips - 1, 1), blocks, half, LANES), f32),
            pltpu.VMEM((blocks, half, LANES), f32),
            pltpu.VMEM((blocks, half, LANES), f32),
            pltpu.SemaphoreType.DMA((2, 2, 2 * shots)),
            pltpu.SemaphoreType.DMA((2, 2, 2 * shots)),
            pltpu.SemaphoreType.DMA((2, 6)),
            pltpu.SemaphoreType.DMA((2, 6)),
            pltpu.SemaphoreType.DMA((chips + 1,)),
            pltpu.SemaphoreType.DMA((chips + 1,)),
        ],
        compiler_params=pltpu.CompilerParams(
            collective_id=0, has_side_effects=True, vmem_limit_bytes=48 * 1024 * 1024
        ),
        name="migrate",
    )(
        wavelet, checkpoint_step, source_depth, source_lateral, courant_sq, sponge_level,
        source_later, source_now, receiver_later, receiver_now, traces, receiver_depth, table,
    )


def solution(mesh):
    in_specs = (
        P(("grp", "slab"), None),
        P(("grp", "slab"), None),
        P(("grp", "shot"), "slab", None),
        P(("grp", "shot"), "slab", None),
        P(("grp", "shot"), "slab", None),
        P(("grp", "shot"), "slab", None),
        P(("grp", "shot"), None, None),
        P("grp"),
        P(("grp", "shot")),
        P(("grp", "shot")),
        P(("grp", "shot"), None),
        P(("grp", "shot"), None),
        P(("grp", "shot")),
    )
    out_specs = (
        P(("grp", "slab"), None),
        P(("grp", "shot"), "slab", None),
        P(("grp", "shot"), "slab", None),
    )
    return jax.shard_map(
        functools.partial(local, mesh.shape["slab"], mesh.shape["shot"]),
        mesh=mesh, in_specs=in_specs, out_specs=out_specs, check_vma=False,
    )
```

time: 275 us -> 75.9 us (0.28)
  Pallas kernels: 0 us -> 65.8 us
  other arithmetic: 63.9 us -> 1.23 us
  waiting for transfers between devices: 56.8 us -> 0 us
  starting transfers between devices: 55.7 us -> 0 us
  matrix products: 50.3 us -> 0 us
  local copies, waits for them, and re-layouts: 31.5 us -> 7.92 us
  between operations: 14.2 us -> 0.72 us
    pallas_call x0 -> x1, Pallas kernels: none -> 65.8 us  [local(): pl.pallas_call(functools.partial(kernel, slabs, shot_devices, 1.0 / math....]
    ppermute x18 -> x0, starting transfers between devices: 55.7 us -> none  [the longest x9 44.1 us: extended_2(): lax.ppermute(tail, axis, [(i, (i + 1) % count) for i in range(ends)])]
    dot_general x16 -> x0, matrix products: 50.3 us -> none  [advance(): jnp.einsum('szr,srx->szx', depth_table, lateral_table, precision=lax.Prec...]
    add x40 -> x0, other arithmetic: 41.2 us -> none  [the longest x16 39.8 us: laplace(): result + stencil_coeffs[offset] * (extended[..., 4 + offset:4 + offset +...]
    psum x1 -> x0, waiting for transfers between devices: 35.4 us -> none  [local(): image_total = lax.psum(carry[4], 'shot')]
    ppermute x18 -> x0, waiting for transfers between devices: 21.3 us -> none  [the longest x9 12.8 us: extended_2(): lax.ppermute(tail, axis, [(i, (i + 1) % count) for i in range(ends)])]
    while x160 -> x0, local copies, waits for them, and re-layouts: 18.2 us -> none
    gather x16 -> x0, local copies, waits for them, and re-layouts: 10.2 us -> none  [advance(): pulse = wavelet[checkpoint_step + STEPS - 1 - step_index]]
  transfers between devices with their start and end apart: 19 -> 0, of which waited for: 19 -> 0; matrix products, arithmetic and copies ran while one was open for 5% -> 0% of each run, Pallas kernels for 0% -> 0%
where the time goes in v1:
time: 75.9 us; the launch traced here: 75.6 us
  Pallas kernels  65.8 us (87%)
  local copies, waits for them, and re-layouts  7.92 us (10%)
  other arithmetic  1.23 us (2%)
    pallas_call x1, Pallas kernels, local(): pl.pallas_call(functools.partial(kernel, slabs, shot_devices, 1.0 / math....  65.8 us
    unnamed x27, local copies, waits for them, and re-layouts  7.92 us

profile of v1, /device:TPU:0, one launch (start us, length us, event | category | flops | bytes accessed | tf_op | source)
XLA Modules:
  0.0 75.6 jit_solution(13665501010827866347)
XLA Ops:
  0.6 0.0 copy-start.7
  0.6 0.0 copy-start.3
  0.7 0.0 copy-start.2
  0.7 0.0 copy-start.1
  0.7 0.0 copy-start
  0.7 1.2 %fusion.table = bf16[2,512,1024]{2,1,0:T(8,128)(2,1)S(1)} fusion(s32[2,512]{1,0:T(2,128)} %param.24), kind=kLoop, calls=%fused_computation.1 | loop fusion | flops 2097152 | bytes 2101248 | tf_op jit(solution)/shard_map/convert_element_type | solution.py:386
  1.9 0.0 copy-done.7
  1.9 0.0 copy-done.3
  1.9 0.0 copy-done.2
  2.0 0.1 copy-done.1
  2.0 0.2 copy-done
  2.2 0.0 copy-start.4
  2.2 0.9 %copy-done.4 = f32[64,1024]{1,0:T(8,128)S(1)} copy-done((f32[64,1024]{1,0:T(8,128)S(1)}, f32[64,1024]{1,0:T(8,128)}, u32[]{:S(2)}) %copy-start.4) | copy-done | bytes 262168
  3.1 0.0 copy-start.5
  3.1 0.9 %copy-done.5 = s32[64,1024]{1,0:T(8,128)S(1)} copy-done((s32[64,1024]{1,0:T(8,128)S(1)}, s32[64,1024]{1,0:T(8,128)}, u32[]{:S(2)}) %copy-start.5) | copy-done | bytes 262168
  4.1 0.0 copy-start.6
  4.1 0.8 %copy-done.6 = f32[2,16,512]{2,1,0:T(8,128)S(1)} copy-done((f32[2,16,512]{2,1,0:T(8,128)S(1)}, f32[2,16,512]{2,1,0:T(8,128)}, u32[]{:S(2)}) %copy-start.6) | copy-done | bytes 65560
  4.9 0.0 copy-start.8
  4.9 0.7 copy-done.8
  5.6 0.0 copy-start.9
  5.6 0.7 copy-done.9
  6.3 0.0 copy-start.10
  6.3 0.7 copy-done.10
  6.9 0.0 copy-start.11
  6.9 0.7 copy-done.11
  7.6 65.8 %migrate.1 = (f32[64,1024]{1,0:T(8,128)S(1)}, f32[2,64,1024]{2,1,0:T(8,128)S(1)}, f32[2,64,1024]{2,1,0:T(8,128)S(1)}) custom-call(f32[256]{0:T(256)S(1)} %copy-done.8, s32[2]{0:T(128)S(1)} %copy-done.9, s32[2]{0:T(128)S(1)} %copy-done.10, s32[2]{0:T(128)S(1)} %copy-done.11, f32[64,1024]{1,0:T(8,128)S(1)} %copy-done.4, s32[64,1024]{1,0:T(8,128)S(1)} %copy-done.5, ...), custom_call_target="tpu_custom_call" | custom-call | tf_op jit(solution)/shard_map/migrate/pallas_call | solution.py:392
  73.3 0.7 copy.19
  74.1 0.8 %copy.20 = f32[2,64,1024]{2,1,0:T(8,128)} copy(f32[2,64,1024]{2,1,0:T(8,128)S(1)} %get-tuple-element.7) | data formatting | bytes 1048576
  74.8 0.8 %copy.21 = f32[2,64,1024]{2,1,0:T(8,128)} copy(f32[2,64,1024]{2,1,0:T(8,128)S(1)} %get-tuple-element.8) | data formatting | bytes 1048576
Async XLA Ops:
  0.6 1.3 %copy-start.7 = (s32[2,512]{1,0:T(2,128)S(1)}, s32[2,512]{1,0:T(2,128)}, u32[]{:S(2)}) copy-start(s32[2,512]{1,0:T(2,128)} %r_depth.1) | copy-start | bytes 12292
  0.6 1.3 %copy-start.3 = (f32[2,64,1024]{2,1,0:T(8,128)S(1)}, f32[2,64,1024]{2,1,0:T(8,128)}, u32[]{:S(2)}) copy-start(f32[2,64,1024]{2,1,0:T(8,128)} %r_now.1) | copy-start | bytes 1572868
  0.7 1.3 %copy-start.2 = (f32[2,64,1024]{2,1,0:T(8,128)S(1)}, f32[2,64,1024]{2,1,0:T(8,128)}, u32[]{:S(2)}) copy-start(f32[2,64,1024]{2,1,0:T(8,128)} %r_later.1) | copy-start | bytes 1572868
  0.7 1.4 %copy-start.1 = (f32[2,64,1024]{2,1,0:T(8,128)S(1)}, f32[2,64,1024]{2,1,0:T(8,128)}, u32[]{:S(2)}) copy-start(f32[2,64,1024]{2,1,0:T(8,128)} %s_now.1) | copy-start | bytes 1572868
  0.7 1.5 %copy-start = (f32[2,64,1024]{2,1,0:T(8,128)S(1)}, f32[2,64,1024]{2,1,0:T(8,128)}, u32[]{:S(2)}) copy-start(f32[2,64,1024]{2,1,0:T(8,128)} %s_later.1) | copy-start | bytes 1572868
  2.2 0.9 %copy-start.4 = (f32[64,1024]{1,0:T(8,128)S(1)}, f32[64,1024]{1,0:T(8,128)}, u32[]{:S(2)}) copy-start(f32[64,1024]{1,0:T(8,128)} %velocity_in.1) | copy-start | bytes 786436
  3.1 0.9 %copy-start.5 = (s32[64,1024]{1,0:T(8,128)S(1)}, s32[64,1024]{1,0:T(8,128)}, u32[]{:S(2)}) copy-start(s32[64,1024]{1,0:T(8,128)} %sponge_in.1) | copy-start | bytes 786436
  4.1 0.8 %copy-start.6 = (f32[2,16,512]{2,1,0:T(8,128)S(1)}, f32[2,16,512]{2,1,0:T(8,128)}, u32[]{:S(2)}) copy-start(f32[2,16,512]{2,1,0:T(8,128)} %traces.1) | copy-start | bytes 196612
  4.9 0.7 copy-start.8
  5.6 0.7 copy-start.9
  6.3 0.7 copy-start.10
  6.9 0.7 copy-start.11
